TPU v7x, 32 devices: a whole 2x2x4 slice. The times are simulated.
32 devices in a mesh: req: 8 (over y, x, core), kv: 4 (over z).
Axes of the slice: x: 2, y: 2, z: 4, core: 2. Of those that a mesh axis runs over, the one named last changes fastest.
Arguments:
- queries: bfloat16 [32, 4096], P(('req', 'kv')), may hold values from -16 to 16
- paged_key_cache: bfloat16 [192, 128, 1024], P(('req', 'kv')), may hold values from -8 to 8
- paged_value_cache: bfloat16 [192, 128, 1024], P(('req', 'kv')), may hold values from -6 to 6
- page_request: int32 [192], P(('req', 'kv')), may hold values from 0 to 31, as said below
- page_number: int32 [192], P(('req', 'kv')), may hold values from 0 to 7, as said below
- lengths: int32 [32], replicated, may hold values from 1 to 1024, as said below
Outputs:
- attended: bfloat16 [32, 4096], P(('req', 'kv'))
Inputs may be any that keep to these rules, and one draw needn't show every extreme that they name: `page_request`: every request has 1 to 8 pages and some request exactly 8; the 6 slots of one device hold pages of requests r with 6 different values of r // 4. `page_number`: the pages of one request are numbered 0, 1, 2 and so on without gaps, each number once. `lengths`: a request with n pages has a length from (n - 1) * 128 + 1 to n * 128.
All inputs are finite; a program needn't handle non-finite values.
Results may differ from a plain program's by a relative error of at most 0.0023.
Values may be sent and summed in bfloat16 or wider, within the bound.
A program may use at most 64 MiB of HBM per device.

v0:
```python
import functools

import jax
import jax.numpy as jnp
from jax import lax
from jax.experimental import pallas as pl
from jax.experimental.pallas import tpu as pltpu
from jax.sharding import PartitionSpec as P

HQ = 32
KEY_VALUE_HEADS = 8
HEAD_SIZE = 128
QUERY_PER_KV = 4
PAIR = 2 * QUERY_PER_KV
STAT = 8

lowest = -1e30
MESH = pl.DeviceIdType.MESH


def partners(me, n):
    if n & (n - 1):
        return [lax.rem(me + d, n) for d in range(n)]
    found = []
    for d in range(n):
        place, bit = me, 1
        while bit < n:
            if d & bit:
                place = place + bit - 2 * bit * lax.rem(lax.div(me, bit), 2)
            bit *= 2
        found.append(place)
    return found


def diagonal_to_lanes(column, on_diagonal):
    return jnp.sum(jnp.where(on_diagonal, column, 0.0), axis=0, keepdims=True)


def lanes_to_column(row, on_diagonal):
    return jnp.sum(jnp.where(on_diagonal, row, 0.0), axis=1, keepdims=True)


def kernel(
    n_req, n_kv, group,
    owner_hbm, number_hbm, length_hbm, q_hbm, key_hbm, value_hbm, out_ref,
    owner_ref, number_ref, length_ref, q_ref, keys, values, q_rows, q_group, table, q_send, q_in, part_send, part_in, merged, merged_in,
    small_sem, page_sem, qs_sem, qr_sem, ts_sem, tr_sem, ds_sem, dr_sem, ps_sem, pr_sem, ms_sem, mr_sem,
):
    slots, page_tokens, _ = keys.shape
    my_req = lax.axis_index("req")
    my_kv = lax.axis_index("kv")

    barrier = pltpu.get_barrier_semaphore()
    req_peers = partners(my_req, n_req)
    kv_peers = partners(my_kv, n_kv)
    for d in range(n_kv - 1, 0, -1):
        pl.semaphore_signal(barrier, inc=1, device_id=(my_req, kv_peers[d]), device_id_type=MESH)
    for d in range(n_req - 1, 0, -1):
        pl.semaphore_signal(barrier, inc=1, device_id=(req_peers[d], my_kv), device_id_type=MESH)

    small = [
        pltpu.make_async_copy(src, dst, small_sem.at[i])
        for i, (src, dst) in enumerate(
            ((q_hbm, q_ref), (owner_hbm, owner_ref), (number_hbm, number_ref), (length_hbm, length_ref))
        )
    ]
    for copy in small:
        copy.start()

    loads = []
    for s in range(slots):
        loads.append(pltpu.make_async_copy(key_hbm.at[s], keys.at[s], page_sem.at[0]))
        loads.append(pltpu.make_async_copy(value_hbm.at[s], values.at[s], page_sem.at[1]))
    for load in loads:
        load.start()
    for copy in small:
        copy.wait()

    for h in range(HQ):
        q_rows[h : h + 1, :] = q_ref[0:1, h * HEAD_SIZE : (h + 1) * HEAD_SIZE].astype(jnp.float32)
    q_group[my_kv] = q_rows[...].astype(jnp.bfloat16)
    lane8 = lax.broadcasted_iota(jnp.int32, (STAT, HEAD_SIZE), 1)
    sub8 = lax.broadcasted_iota(jnp.int32, (STAT, HEAD_SIZE), 0)
    own_table = jnp.full((STAT, HEAD_SIZE), -1.0, jnp.float32)
    for s in range(slots):
        own_table = jnp.where(lane8 == s, owner_ref[s].astype(jnp.float32), own_table)
    table[my_req] = own_table

    pl.semaphore_wait(barrier, n_req - 1 + n_kv - 1)

    def remote(src, dst, send, recv, target):
        return pltpu.make_async_remote_copy(
            src_ref=src, dst_ref=dst, send_sem=send, recv_sem=recv,
            device_id=target, device_id_type=MESH,
        )

    def arrived(buffer, count, sem):
        if count:
            pltpu.make_async_copy(buffer.at[pl.ds(0, count)], buffer.at[pl.ds(0, count)], sem).wait()

    for d in range(n_kv - 1, 0, -1):
        copy = remote(q_group.at[my_kv], q_group.at[my_kv], qs_sem.at[0], qr_sem.at[0], (my_req, kv_peers[d]))
        copy.start()
    for d in range(n_req - 1, 0, -1):
        copy = remote(table.at[my_req], table.at[my_req], ts_sem.at[0], tr_sem.at[0], (req_peers[d], my_kv))
        copy.start()

    homes = []
    for d in range(n_req):
        index, present = jnp.int32(0), jnp.int32(0)
        for s in range(slots):
            same = lax.div(owner_ref[s], group) == req_peers[d]
            index = jnp.where(same, jnp.int32(s), index)
            present = jnp.where(same, jnp.int32(1), present)
        limit = length_ref[owner_ref[index]] - number_ref[index] * page_tokens
        homes.append((index, limit * present))

    arrived(table, n_req - 1, tr_sem.at[0])
    base = (my_req * group).astype(jnp.float32)
    held = []
    for d in range(n_req):
        rel = table[req_peers[d]] - base
        inside = jnp.logical_and(rel >= 0.0, rel < float(group))
        held.append(jnp.max(jnp.where(inside, rel, -1.0), axis=1, keepdims=True)[0:1])
    arrived(q_group, n_kv - 1, qr_sem.at[0])

    choices = [q_group[c].astype(jnp.float32) for c in range(group)]
    edges = [0, max(n_req // 4, 1), max(3 * n_req // 4, 1), n_req]
    stage_of = [sum(d >= edge for edge in edges[1:]) for d in range(n_req)]
    for d in list(range(n_req - 1, -1, -1)):
        pick = jnp.broadcast_to(held[d], (HQ, HEAD_SIZE))
        chosen = jnp.zeros((HQ, HEAD_SIZE), jnp.float32)
        for c in range(group):
            chosen = jnp.where(pick == float(c), choices[c], chosen)
        if d == 0:
            q_in[my_req] = chosen.astype(jnp.bfloat16)
            continue
        q_send[d] = chosen.astype(jnp.bfloat16)
        copy = remote(q_send.at[d], q_in.at[my_req], ds_sem.at[0], dr_sem.at[stage_of[d]], (req_peers[d], my_kv))
        copy.start()

    pltpu.make_async_copy(key_hbm, keys, page_sem.at[0]).wait()
    pltpu.make_async_copy(value_hbm, values, page_sem.at[1]).wait()

    row = lax.broadcasted_iota(jnp.int32, (HQ, HEAD_SIZE), 0)
    lane = lax.broadcasted_iota(jnp.int32, (HQ, HEAD_SIZE), 1)
    on_diagonal = row == lane
    first = sub8 < QUERY_PER_KV
    token = lax.broadcasted_iota(jnp.int32, (HQ, page_tokens), 1)
    wide = 2 * HEAD_SIZE

    for stage, (low, high) in enumerate(zip(edges[:-1], edges[1:])):
        batch = range(high - 1, low - 1, -1)
        arrived(q_in, high - max(low, 1), dr_sem.at[stage])
        scored = {}
        for d in batch:
            index, limit = homes[d]
            query = q_in[req_peers[d]].astype(jnp.float32)
            pieces = []
            for k in range(HQ // PAIR):
                q8 = query[k * PAIR : (k + 1) * PAIR]
                both = jnp.concatenate(
                    [jnp.where(first, q8, 0.0), jnp.where(first, 0.0, q8)], axis=1
                ).astype(jnp.bfloat16)
                pieces.append(
                    lax.dot_general(
                        both, keys[index, :, k * wide : (k + 1) * wide],
                        (((1,), (1,)), ((), ())), preferred_element_type=jnp.float32,
                    )
                )
            scores = jnp.concatenate(pieces, axis=0) * HEAD_SIZE ** (-0.5)
            scored[d] = jnp.where(token < limit, scores, lowest)
        tops = {d: jnp.max(scored[d], axis=1, keepdims=True) for d in batch}
        weights = {d: jnp.exp(scored[d] - tops[d]) for d in batch}
        totals = {d: jnp.sum(weights[d], axis=1, keepdims=True) for d in batch}
        for d in batch:
            index, limit = homes[d]
            blocks = []
            for k in range(HQ // PAIR):
                w8 = weights[d][k * PAIR : (k + 1) * PAIR].astype(jnp.bfloat16)
                both = jnp.dot(
                    w8, values[index, :, k * wide : (k + 1) * wide], preferred_element_type=jnp.float32
                )
                blocks.append(jnp.where(first, both[:, :HEAD_SIZE], both[:, HEAD_SIZE:]))
            blocks.append(diagonal_to_lanes(tops[d], on_diagonal))
            blocks.append(diagonal_to_lanes(totals[d], on_diagonal))
            block = jnp.concatenate(blocks, axis=0)
            if d == 0:
                part_in[my_req] = block
                continue
            part_send[d] = block
            copy = remote(part_send.at[d], part_in.at[my_req], ps_sem.at[0], pr_sem.at[0], (req_peers[d], my_kv))
            copy.start()
    arrived(part_in, n_req - 1, pr_sem.at[0])

    tops, totals = [], []
    for d in range(n_req):
        tops.append(part_in[req_peers[d], HQ : HQ + 1, :])
        totals.append(part_in[req_peers[d], HQ + 1 : HQ + 2, :])
    merged_top, merged_total = [], []
    factors = [jnp.zeros((1, HEAD_SIZE), jnp.float32) for _ in range(n_req)]
    member = [[jnp.broadcast_to(held[d], (1, HEAD_SIZE)) == float(c) for d in range(n_req)] for c in range(group)]
    for c in range(group):
        best = jnp.full((1, HEAD_SIZE), lowest, jnp.float32)
        for d in range(n_req):
            best = jnp.maximum(best, jnp.where(member[c][d], tops[d], lowest))
        merged_top.append(best)
    for d in range(n_req):
        best = tops[d]
        for c in range(group):
            best = jnp.where(member[c][d], merged_top[c], best)
        factors[d] = jnp.exp(tops[d] - best)
    for c in range(group):
        amount = jnp.zeros((1, HEAD_SIZE), jnp.float32)
        for d in range(n_req):
            amount = amount + jnp.where(member[c][d], factors[d] * totals[d], 0.0)
        merged_total.append(amount)
    sums = [jnp.zeros((HQ, HEAD_SIZE), jnp.float32) for _ in range(group)]
    for d in range(n_req):
        scaled = lanes_to_column(factors[d], on_diagonal) * part_in[req_peers[d], 0:HQ, :]
        pick = jnp.broadcast_to(held[d], (HQ, HEAD_SIZE))
        for c in range(group):
            sums[c] = sums[c] + jnp.where(pick == float(c), scaled, 0.0)
    for c in range(group):
        merged[c, 0:HQ, :] = sums[c]
        merged[c, HQ : HQ + 2, :] = jnp.concatenate([merged_top[c], merged_total[c]], axis=0)

    for d in range(n_kv - 1, 0, -1):
        copy = remote(merged.at[kv_peers[d]], merged_in.at[my_kv], ms_sem.at[0], mr_sem.at[0], (my_req, kv_peers[d]))
        copy.start()
    merged_in[my_kv] = merged[my_kv]
    arrived(merged_in, n_kv - 1, mr_sem.at[0])

    tops = [merged_in[c, HQ : HQ + 1, :] for c in range(n_kv)]
    best = tops[0]
    for c in range(1, n_kv):
        best = jnp.maximum(best, tops[c])
    factors = [jnp.exp(tops[c] - best) for c in range(n_kv)]
    amount = jnp.zeros((1, HEAD_SIZE), jnp.float32)
    for c in range(n_kv):
        amount = amount + factors[c] * merged_in[c, HQ + 1 : HQ + 2, :]
    result = jnp.zeros((HQ, HEAD_SIZE), jnp.float32)
    for c in range(n_kv):
        result = result + lanes_to_column(factors[c], on_diagonal) * merged_in[c, 0:HQ, :]
    result = result / lanes_to_column(amount, on_diagonal)
    out_ref[...] = result.astype(jnp.bfloat16)

    arrived(q_group, n_kv - 1, qs_sem.at[0])
    arrived(table, n_req - 1, ts_sem.at[0])
    arrived(q_send, n_req - 1, ds_sem.at[0])
    arrived(part_send, n_req - 1, ps_sem.at[0])
    arrived(merged, n_kv - 1, ms_sem.at[0])


def solution(mesh):
    n_req, n_kv = mesh.shape["req"], mesh.shape["kv"]

    def on_device(queries, key_cache, value_cache, page_request, page_number, lengths):
        slots, page_tokens, width = key_cache.shape
        group = lengths.shape[0] // n_req
        dma = pltpu.SemaphoreType.DMA
        vmem = pl.BlockSpec(memory_space=pltpu.VMEM)
        anywhere = pl.BlockSpec(memory_space=pl.ANY)
        blob = (HQ + 2, HEAD_SIZE)
        attended = pl.pallas_call(
            functools.partial(kernel, n_req, n_kv, group),
            out_shape=pltpu.VMEM((HQ, HEAD_SIZE), jnp.bfloat16),
            in_specs=[anywhere] * 6,
            out_specs=vmem,
            scratch_shapes=[
                pltpu.SMEM(page_request.shape, jnp.int32),
                pltpu.SMEM(page_number.shape, jnp.int32),
                pltpu.SMEM(lengths.shape, jnp.int32),
                pltpu.VMEM(queries.shape, queries.dtype),
                pltpu.VMEM((slots, page_tokens, width), jnp.bfloat16),
                pltpu.VMEM((slots, page_tokens, width), jnp.bfloat16),
                pltpu.VMEM((HQ, HEAD_SIZE), jnp.float32),
                pltpu.VMEM((n_kv, HQ, HEAD_SIZE), jnp.bfloat16),
                pltpu.VMEM((n_req, STAT, HEAD_SIZE), jnp.float32),
                pltpu.VMEM((n_req, HQ, HEAD_SIZE), jnp.bfloat16),
                pltpu.VMEM((n_req, HQ, HEAD_SIZE), jnp.bfloat16),
                pltpu.VMEM((n_req,) + blob, jnp.float32),
                pltpu.VMEM((n_req,) + blob, jnp.float32),
                pltpu.VMEM((group,) + blob, jnp.float32),
                pltpu.VMEM((n_kv,) + blob, jnp.float32),
                dma((4,)),
                dma((2,)),
                dma((1,)), dma((1,)),
                dma((1,)), dma((1,)),
                dma((1,)), dma((3,)),
                dma((1,)), dma((1,)),
                dma((1,)), dma((1,)),
            ],
            compiler_params=pltpu.CompilerParams(collective_id=0, has_side_effects=True),
        )(page_request, page_number, lengths, queries, key_cache, value_cache)
        return attended.reshape(queries.shape)

    placed = (
        P(("req", "kv"), None),
        P(("req", "kv"), None, None),
        P(("req", "kv"), None, None),
        P(("req", "kv")),
        P(("req", "kv")),
        P(),
    )
    return jax.shard_map(
        on_device, mesh=mesh, in_specs=placed, out_specs=P(("req", "kv"), None), check_vma=False
    )
```

profile of v0, /device:TPU:0, one launch (start us, length us, event | category | flops | bytes accessed | tf_op | source)
XLA Modules:
  0.0 21.4 jit_solution(5199194563913930680)
XLA Ops:
  0.0 20.8 %shard_map.64 = bf16[32,128]{1,0:T(8,128)(2,1)S(1)} custom-call(s32[6]{0:T(128)} %owner_hbm.1, s32[6]{0:T(128)} %number_hbm.1, s32[32]{0:T(128)} %length_hbm.1, bf16[1,4096]{1,0:T(2,128)(2,1)} %q_hbm.1, bf16[6,128,1024]{2,1,0:T(8,128)(2,1)} %key_hbm.1, bf16[6,128,1024]{2,1,0:T(8,128)(2,1)} %value_hbm.1), custom_call_target="tpu_custom_call" | custom-call | tf_op jit(solution)/shard_map/pallas_call | solution.py:265
  20.8 0.6 %copy.9 = bf16[1,1,32,128]{3,1,2,0:T(2,128)(2,1)} copy(bf16[1,1,32,128]{3,2,1,0:T(8,128)(2,1)S(1)} %bitcast.5) | data formatting | bytes 16384
where the time goes:
time: 21.6 us; the launch traced here: 21.4 us
  Pallas kernels  20.8 us (96%)
  local copies, waits for them, and re-layouts  0.62 us (3%)
    pallas_call x1, Pallas kernels, on_device(): pl.pallas_call(functools.partial(kernel, n_req, n_kv, group), out_shape=p...  20.8 us
    unnamed x1, local copies, waits for them, and re-layouts  0.62 us

commit v1 on v0

v1 whole, which is shorter than its diff:
```python
import functools

import jax
import jax.numpy as jnp
from jax import lax
from jax.experimental import pallas as pl
from jax.experimental.pallas import tpu as pltpu
from jax.sharding import PartitionSpec as P

HQ = 32
KEY_VALUE_HEADS = 8
HEAD_SIZE = 128
QUERY_PER_KV = 4
CORES = 2
PAIR = 2 * QUERY_PER_KV

lowest = -1e30
MESH = pl.DeviceIdType.MESH


def partners(me, n):
    if n & (n - 1):
        return [lax.rem(me + d, n) for d in range(n)]
    found = []
    for d in range(n):
        place, bit = me, 1
        while bit < n:
            if d & bit:
                place = place + bit - 2 * bit * lax.rem(lax.div(me, bit), 2)
            bit *= 2
        found.append(place)
    return found


def diagonal_to_lanes(column, on_diagonal):
    return jnp.sum(jnp.where(on_diagonal, column, 0.0), axis=0, keepdims=True)


def lanes_to_column(row, on_diagonal):
    return jnp.sum(jnp.where(on_diagonal, row, 0.0), axis=1, keepdims=True)


def kernel(
    n_req, n_kv, group,
    owner_hbm, number_hbm, length_hbm, q_hbm, key_hbm, value_hbm, out_ref,
    owner_ref, number_ref, length_ref, q_ref, keys, values, q_rows, q_own, q_col, table, held, q_send, q_in,
    part_send, part_in, merged, merged_in,
    small_sem, page_sem, qs_sem, qr_sem, ts_sem, tr_sem, ds_sem, dr_sem, ps_sem, pr_sem, ms_sem, mr_sem,
):
    slots, page_tokens, _ = keys.shape
    n_chip = n_req // CORES
    my_req = lax.axis_index("req")
    my_kv = lax.axis_index("kv")
    my_chip = lax.div(my_req, CORES)
    core = lax.rem(my_req, CORES)
    is_hub = core == CORES - 1
    is_leaf = core < CORES - 1
    chip_peers = partners(my_chip, n_chip)
    kv_peers = partners(my_kv, n_kv)
    hub_of = [CORES * chip + CORES - 1 for chip in chip_peers]
    leaf_of = [CORES * chip for chip in chip_peers]

    barrier = pltpu.get_barrier_semaphore()

    @pl.when(is_hub)
    def _():
        for d in range(n_kv - 1, 0, -1):
            pl.semaphore_signal(barrier, inc=1, device_id=(hub_of[0], kv_peers[d]), device_id_type=MESH)
        for d in range(n_chip - 1, 0, -1):
            pl.semaphore_signal(barrier, inc=1, device_id=(hub_of[d], my_kv), device_id_type=MESH)
            pl.semaphore_signal(barrier, inc=1, device_id=(leaf_of[d], my_kv), device_id_type=MESH)
        for d in range(n_kv - 1, -1, -1):
            pl.semaphore_signal(barrier, inc=1, device_id=(leaf_of[0], kv_peers[d]), device_id_type=MESH)

    small = [
        pltpu.make_async_copy(src, dst, small_sem.at[i])
        for i, (src, dst) in enumerate(
            ((owner_hbm, owner_ref), (q_hbm, q_ref), (number_hbm, number_ref), (length_hbm, length_ref))
        )
    ]
    for copy in small:
        copy.start()
    for s in range(slots):
        pltpu.make_async_copy(key_hbm.at[s], keys.at[s], page_sem.at[0]).start()
        pltpu.make_async_copy(value_hbm.at[s], values.at[s], page_sem.at[1]).start()

    def remote(src, dst, send, recv, target):
        return pltpu.make_async_remote_copy(
            src_ref=src, dst_ref=dst, send_sem=send, recv_sem=recv,
            device_id=target, device_id_type=MESH,
        )

    def arrived(buffer, count, sem):
        if count:
            pltpu.make_async_copy(buffer.at[pl.ds(0, count)], buffer.at[pl.ds(0, count)], sem).wait()

    small[0].wait()
    lane1 = lax.broadcasted_iota(jnp.int32, (1, HEAD_SIZE), 1)
    own_table = jnp.full((1, HEAD_SIZE), -1.0, jnp.float32)
    for s in range(slots):
        own_table = jnp.where(lane1 == s, owner_ref[s].astype(jnp.float32), own_table)
    table[my_req] = own_table
    small[1].wait()
    for h in range(HQ):
        q_rows[h : h + 1, :] = q_ref[0:1, h * HEAD_SIZE : (h + 1) * HEAD_SIZE].astype(jnp.float32)
    own_query = q_rows[...].astype(jnp.bfloat16)
    q_own[...] = own_query
    small[2].wait()
    small[3].wait()

    pl.semaphore_wait(barrier, n_kv + n_chip - 1 - core)

    mine = core * n_kv + my_kv
    for d in range(n_chip - 1, 0, -1):
        remote(table.at[my_req], table.at[my_req], ts_sem.at[0], tr_sem.at[0], (hub_of[d], my_kv)).start()
    for d in range(n_kv - 1, 0, -1):
        remote(q_own, q_col.at[mine], qs_sem.at[0], qr_sem.at[0], (hub_of[0], kv_peers[d])).start()

    @pl.when(is_leaf)
    def _():
        remote(table.at[my_req], table.at[my_req], ts_sem.at[0], tr_sem.at[0], (hub_of[0], my_kv)).start()
        remote(q_own, q_col.at[mine], qs_sem.at[0], qr_sem.at[0], (hub_of[0], my_kv)).start()

    homes = []
    for d in range(n_chip):
        pair = []
        for b in range(CORES):
            index, present = jnp.int32(0), jnp.int32(0)
            for s in range(slots):
                same = lax.div(owner_ref[s], group) == leaf_of[d] + b
                index = jnp.where(same, jnp.int32(s), index)
                present = jnp.where(same, jnp.int32(1), present)
            limit = length_ref[owner_ref[index]] - number_ref[index] * page_tokens
            pair.append((index, limit * present))
        homes.append(pair)

    edges = [0, max(n_chip // 4, 1), max(3 * n_chip // 4, 1), n_chip]
    stage_of = [sum(d >= edge for edge in edges[1:]) for d in range(n_chip)]

    @pl.when(is_hub)
    def _():
        q_col[(CORES - 1) * n_kv + my_kv] = q_own[...]
        arrived(table, n_req - 1, tr_sem.at[0])
        picks = {}
        for d in range(n_chip - 1, -1, -1):
            for a in range(CORES):
                row = table[leaf_of[d] + a]
                for b in range(CORES):
                    rel = row - ((leaf_of[0] + b) * group).astype(jnp.float32)
                    inside = jnp.logical_and(rel >= 0.0, rel < float(group))
                    picks[d, a, b] = jnp.max(jnp.where(inside, rel, -1.0), axis=1, keepdims=True)
        for (d, a, b), pick in picks.items():
            held[b, d * CORES + a] = jnp.broadcast_to(pick, (1, HEAD_SIZE))
        arrived(q_col, CORES * n_kv - 1, qr_sem.at[0])
        choices = [q_col[c].astype(jnp.float32) for c in range(CORES * group)]
        for d in range(n_chip - 1, -1, -1):
            for a in range(CORES):
                for b in range(CORES):
                    pick = jnp.broadcast_to(picks[d, a, b], (HQ, HEAD_SIZE))
                    chosen = jnp.zeros((HQ, HEAD_SIZE), jnp.float32)
                    for c in range(group):
                        chosen = jnp.where(pick == float(c), choices[b * group + c], chosen)
                    if d == 0 and a == CORES - 1:
                        q_in[my_chip, b] = chosen.astype(jnp.bfloat16)
                    else:
                        q_send[d * CORES + a, b] = chosen.astype(jnp.bfloat16)
                if d or a < CORES - 1:
                    remote(
                        q_send.at[d * CORES + a], q_in.at[my_chip], ds_sem.at[0], dr_sem.at[stage_of[d]],
                        (leaf_of[d] + a, my_kv),
                    ).start()

    pltpu.make_async_copy(key_hbm, keys, page_sem.at[0]).wait()
    pltpu.make_async_copy(value_hbm, values, page_sem.at[1]).wait()

    row = lax.broadcasted_iota(jnp.int32, (HQ, HEAD_SIZE), 0)
    lane = lax.broadcasted_iota(jnp.int32, (HQ, HEAD_SIZE), 1)
    on_diagonal = row == lane
    first = lax.broadcasted_iota(jnp.int32, (PAIR, HEAD_SIZE), 0) < QUERY_PER_KV
    token = lax.broadcasted_iota(jnp.int32, (HQ, page_tokens), 1)
    wide = 2 * HEAD_SIZE

    for stage, (low, high) in enumerate(zip(edges[:-1], edges[1:])):
        batch = [(d, b) for d in range(high - 1, low - 1, -1) for b in range(CORES)]
        if low == 0:

            @pl.when(is_leaf)
            def _():
                arrived(q_in, 1, dr_sem.at[0])

        arrived(q_in, high - max(low, 1), dr_sem.at[stage])
        scored = {}
        for d, b in batch:
            index, limit = homes[d][b]
            query = q_in[chip_peers[d], b].astype(jnp.float32)
            pieces = []
            for k in range(HQ // PAIR):
                q8 = query[k * PAIR : (k + 1) * PAIR]
                both = jnp.concatenate(
                    [jnp.where(first, q8, 0.0), jnp.where(first, 0.0, q8)], axis=1
                ).astype(jnp.bfloat16)
                pieces.append(
                    lax.dot_general(
                        both, keys[index, :, k * wide : (k + 1) * wide],
                        (((1,), (1,)), ((), ())), preferred_element_type=jnp.float32,
                    )
                )
            scores = jnp.concatenate(pieces, axis=0) * HEAD_SIZE ** (-0.5)
            scored[d, b] = jnp.where(token < limit, scores, lowest)
        tops = {e: jnp.max(scored[e], axis=1, keepdims=True) for e in batch}
        weights = {e: jnp.exp(scored[e] - tops[e]) for e in batch}
        totals = {e: jnp.sum(weights[e], axis=1, keepdims=True) for e in batch}
        for d, b in batch:
            index, limit = homes[d][b]
            blocks = []
            for k in range(HQ // PAIR):
                w8 = weights[d, b][k * PAIR : (k + 1) * PAIR].astype(jnp.bfloat16)
                both = jnp.dot(
                    w8, values[index, :, k * wide : (k + 1) * wide], preferred_element_type=jnp.float32
                )
                blocks.append(jnp.where(first, both[:, :HEAD_SIZE], both[:, HEAD_SIZE:]))
            blocks.append(diagonal_to_lanes(tops[d, b], on_diagonal))
            blocks.append(diagonal_to_lanes(totals[d, b], on_diagonal))
            part_send[d, b] = jnp.concatenate(blocks, axis=0)
            if b < CORES - 1:
                continue
            copy = remote(part_send.at[d], part_in.at[my_req], ps_sem.at[0], pr_sem.at[0], (hub_of[d], my_kv))
            if d == 0:
                pl.when(is_leaf)(copy.start)
            else:
                copy.start()

    @pl.when(is_hub)
    def _():
        arrived(part_in, n_req - 1, pr_sem.at[0])
        for b in range(CORES):
            sources = []
            for d in range(n_chip):
                for a in range(CORES):
                    if d == 0 and a == CORES - 1:
                        sources.append(part_send.at[0, b])
                    else:
                        sources.append(part_in.at[leaf_of[d] + a, b])
            tops = [source[HQ : HQ + 1, :] for source in sources]
            totals = [source[HQ + 1 : HQ + 2, :] for source in sources]
            picks = [held[b, e] for e in range(n_req)]
            member = [[picks[e] == float(c) for e in range(n_req)] for c in range(group)]
            merged_top, merged_total = [], []
            for c in range(group):
                best = jnp.full((1, HEAD_SIZE), lowest, jnp.float32)
                for e in range(n_req):
                    best = jnp.maximum(best, jnp.where(member[c][e], tops[e], lowest))
                merged_top.append(best)
            factors = []
            for e in range(n_req):
                best = tops[e]
                for c in range(group):
                    best = jnp.where(member[c][e], merged_top[c], best)
                factors.append(jnp.exp(tops[e] - best))
            for c in range(group):
                amount = jnp.zeros((1, HEAD_SIZE), jnp.float32)
                for e in range(n_req):
                    amount = amount + jnp.where(member[c][e], factors[e] * totals[e], 0.0)
                merged_total.append(amount)
            sums = [jnp.zeros((HQ, HEAD_SIZE), jnp.float32) for _ in range(group)]
            for e in range(n_req):
                scaled = lanes_to_column(factors[e], on_diagonal) * sources[e][0:HQ, :]
                pick = jnp.broadcast_to(picks[e], (HQ, HEAD_SIZE))
                for c in range(group):
                    sums[c] = sums[c] + jnp.where(pick == float(c), scaled, 0.0)
            for c in range(group):
                merged[b * n_kv + c, 0:HQ, :] = sums[c]
                merged[b * n_kv + c, HQ : HQ + 2, :] = jnp.concatenate([merged_top[c], merged_total[c]], axis=0)
            for d in range(n_kv - 1, -1, -1):
                if d == 0 and b == CORES - 1:
                    merged_in[my_kv] = merged[b * n_kv + my_kv]
                    continue
                remote(
                    merged.at[b * n_kv + kv_peers[d]], merged_in.at[my_kv], ms_sem.at[0], mr_sem.at[0],
                    (leaf_of[0] + b, kv_peers[d]),
                ).start()

    @pl.when(is_leaf)
    def _():
        arrived(merged_in, n_kv, mr_sem.at[0])

    @pl.when(is_hub)
    def _():
        arrived(merged_in, n_kv - 1, mr_sem.at[0])

    tops = [merged_in[c, HQ : HQ + 1, :] for c in range(n_kv)]
    best = tops[0]
    for c in range(1, n_kv):
        best = jnp.maximum(best, tops[c])
    factors = [jnp.exp(tops[c] - best) for c in range(n_kv)]
    amount = jnp.zeros((1, HEAD_SIZE), jnp.float32)
    for c in range(n_kv):
        amount = amount + factors[c] * merged_in[c, HQ + 1 : HQ + 2, :]
    result = jnp.zeros((HQ, HEAD_SIZE), jnp.float32)
    for c in range(n_kv):
        result = result + lanes_to_column(factors[c], on_diagonal) * merged_in[c, 0:HQ, :]
    result = result / lanes_to_column(amount, on_diagonal)
    out_ref[...] = result.astype(jnp.bfloat16)

    @pl.when(is_leaf)
    def _():
        arrived(q_col, n_kv, qs_sem.at[0])
        arrived(table, n_chip, ts_sem.at[0])
        arrived(part_send, n_chip, ps_sem.at[0])

    @pl.when(is_hub)
    def _():
        arrived(q_col, n_kv - 1, qs_sem.at[0])
        arrived(table, n_chip - 1, ts_sem.at[0])
        arrived(part_send, n_chip - 1, ps_sem.at[0])
        arrived(q_send, n_req - 1, ds_sem.at[0])
        arrived(merged, CORES * n_kv - 1, ms_sem.at[0])


def solution(mesh):
    n_req, n_kv = mesh.shape["req"], mesh.shape["kv"]

    def on_device(queries, key_cache, value_cache, page_request, page_number, lengths):
        slots, page_tokens, width = key_cache.shape
        group = lengths.shape[0] // n_req
        n_chip = n_req // CORES
        dma = pltpu.SemaphoreType.DMA
        vmem = pl.BlockSpec(memory_space=pltpu.VMEM)
        anywhere = pl.BlockSpec(memory_space=pl.ANY)
        blob = (HQ + 2, HEAD_SIZE)
        attended = pl.pallas_call(
            functools.partial(kernel, n_req, n_kv, group),
            out_shape=pltpu.VMEM((HQ, HEAD_SIZE), jnp.bfloat16),
            in_specs=[anywhere] * 6,
            out_specs=vmem,
            scratch_shapes=[
                pltpu.SMEM(page_request.shape, jnp.int32),
                pltpu.SMEM(page_number.shape, jnp.int32),
                pltpu.SMEM(lengths.shape, jnp.int32),
                pltpu.VMEM(queries.shape, queries.dtype),
                pltpu.VMEM((slots, page_tokens, width), jnp.bfloat16),
                pltpu.VMEM((slots, page_tokens, width), jnp.bfloat16),
                pltpu.VMEM((HQ, HEAD_SIZE), jnp.float32),
                pltpu.VMEM((HQ, HEAD_SIZE), jnp.bfloat16),
                pltpu.VMEM((CORES * n_kv, HQ, HEAD_SIZE), jnp.bfloat16),
                pltpu.VMEM((n_req, 1, HEAD_SIZE), jnp.float32),
                pltpu.VMEM((CORES, n_req, 1, HEAD_SIZE), jnp.float32),
                pltpu.VMEM((n_req, CORES, HQ, HEAD_SIZE), jnp.bfloat16),
                pltpu.VMEM((n_chip, CORES, HQ, HEAD_SIZE), jnp.bfloat16),
                pltpu.VMEM((n_chip, CORES) + blob, jnp.float32),
                pltpu.VMEM((n_req, CORES) + blob, jnp.float32),
                pltpu.VMEM((CORES * n_kv,) + blob, jnp.float32),
                pltpu.VMEM((n_kv,) + blob, jnp.float32),
                dma((4,)),
                dma((2,)),
                dma((1,)), dma((1,)),
                dma((1,)), dma((1,)),
                dma((1,)), dma((3,)),
                dma((1,)), dma((1,)),
                dma((1,)), dma((1,)),
            ],
            compiler_params=pltpu.CompilerParams(collective_id=0, has_side_effects=True),
        )(page_request, page_number, lengths, queries, key_cache, value_cache)
        return attended.reshape(queries.shape)

    placed = (
        P(("req", "kv"), None),
        P(("req", "kv"), None, None),
        P(("req", "kv"), None, None),
        P(("req", "kv")),
        P(("req", "kv")),
        P(),
    )
    return jax.shard_map(
        on_device, mesh=mesh, in_specs=placed, out_specs=P(("req", "kv"), None), check_vma=False
    )
```

time: 21.6 us -> 19.5 us (0.903)
  Pallas kernels: 20.8 us -> 18.7 us
    pallas_call x1, Pallas kernels: 20.8 us -> 18.7 us  [on_device(): pl.pallas_call(functools.partial(kernel, n_req, n_kv, group), out_shape=p...]
where the time goes in v1:
time: 19.5 us; the launch traced here: 19.4 us
  Pallas kernels  18.7 us (96%)
  local copies, waits for them, and re-layouts  0.62 us (3%)
    pallas_call x1, Pallas kernels, on_device(): pl.pallas_call(functools.partial(kernel, n_req, n_kv, group), out_shape=p...  18.7 us
    unnamed x1, local copies, waits for them, and re-layouts  0.62 us

profile of v1, /device:TPU:0, one launch (start us, length us, event | category | flops | bytes accessed | tf_op | source)
XLA Modules:
  0.0 19.4 jit_solution(6045009137051093160)
XLA Ops:
  0.0 18.7 %shard_map.64 = bf16[32,128]{1,0:T(8,128)(2,1)S(1)} custom-call(s32[6]{0:T(128)} %owner_hbm.1, s32[6]{0:T(128)} %number_hbm.1, s32[32]{0:T(128)} %length_hbm.1, bf16[1,4096]{1,0:T(2,128)(2,1)} %q_hbm.1, bf16[6,128,1024]{2,1,0:T(8,128)(2,1)} %key_hbm.1, bf16[6,128,1024]{2,1,0:T(8,128)(2,1)} %value_hbm.1), custom_call_target="tpu_custom_call" | custom-call | tf_op jit(solution)/shard_map/pallas_call | solution.py:331
  18.8 0.6 %copy.9 = bf16[1,1,32,128]{3,1,2,0:T(2,128)(2,1)} copy(bf16[1,1,32,128]{3,2,1,0:T(8,128)(2,1)S(1)} %bitcast.5) | data formatting | bytes 16384

commit v2 on v1

--- a/solution.py
+++ b/solution.py
@@ -15,6 +15,8 @@
 PAIR = 2 * QUERY_PER_KV
 
 lowest = -1e30
+finest = 1e-30
+STEPS = 32767.0
 MESH = pl.DeviceIdType.MESH
 
 
@@ -44,33 +46,24 @@
     n_req, n_kv, group,
     owner_hbm, number_hbm, length_hbm, q_hbm, key_hbm, value_hbm, out_ref,
     owner_ref, number_ref, length_ref, q_ref, keys, values, q_rows, q_own, q_col, table, held, q_send, q_in,
-    part_send, part_in, merged, merged_in,
-    small_sem, page_sem, qs_sem, qr_sem, ts_sem, tr_sem, ds_sem, dr_sem, ps_sem, pr_sem, ms_sem, mr_sem,
+    part_send, part_in, stat_send, stat_in, near_send, near_in, near_stat, merged, merged_in,
+    met_sem, small_sem, page_sem, qs_sem, qr_sem, ts_sem, tr_sem, ds_sem, dr_sem, ps_sem, pr_sem, ss_sem, sr_sem, ns_sem, nr_sem, ms_sem, mr_sem,
 ):
     slots, page_tokens, _ = keys.shape
     n_chip = n_req // CORES
+    n_near = n_chip
     my_req = lax.axis_index("req")
     my_kv = lax.axis_index("kv")
     my_chip = lax.div(my_req, CORES)
     core = lax.rem(my_req, CORES)
     is_hub = core == CORES - 1
     is_leaf = core < CORES - 1
+    is_last = my_kv == n_kv - 1
+    is_near = jnp.logical_and(my_kv == 0, my_chip < n_near)
     chip_peers = partners(my_chip, n_chip)
     kv_peers = partners(my_kv, n_kv)
     hub_of = [CORES * chip + CORES - 1 for chip in chip_peers]
     leaf_of = [CORES * chip for chip in chip_peers]
-
-    barrier = pltpu.get_barrier_semaphore()
-
-    @pl.when(is_hub)
-    def _():
-        for d in range(n_kv - 1, 0, -1):
-            pl.semaphore_signal(barrier, inc=1, device_id=(hub_of[0], kv_peers[d]), device_id_type=MESH)
-        for d in range(n_chip - 1, 0, -1):
-            pl.semaphore_signal(barrier, inc=1, device_id=(hub_of[d], my_kv), device_id_type=MESH)
-            pl.semaphore_signal(barrier, inc=1, device_id=(leaf_of[d], my_kv), device_id_type=MESH)
-        for d in range(n_kv - 1, -1, -1):
-            pl.semaphore_signal(barrier, inc=1, device_id=(leaf_of[0], kv_peers[d]), device_id_type=MESH)
 
     small = [
         pltpu.make_async_copy(src, dst, small_sem.at[i])
@@ -78,11 +71,21 @@
             ((owner_hbm, owner_ref), (q_hbm, q_ref), (number_hbm, number_ref), (length_hbm, length_ref))
         )
     ]
-    for copy in small:
+    for copy in small[:2]:
         copy.start()
-    for s in range(slots):
-        pltpu.make_async_copy(key_hbm.at[s], keys.at[s], page_sem.at[0]).start()
-        pltpu.make_async_copy(value_hbm.at[s], values.at[s], page_sem.at[1]).start()
+
+    barrier = pltpu.get_barrier_semaphore()
+
+    @pl.when(is_hub)
+    def _():
+        for d in range(n_kv - 1, -1, -1):
+            pl.semaphore_signal(barrier, inc=1, device_id=(leaf_of[0], kv_peers[d]), device_id_type=MESH)
+        for d in range(n_chip - 1, 0, -1):
+            pl.semaphore_signal(barrier, inc=1, device_id=(hub_of[d], my_kv), device_id_type=MESH)
+
+    @pl.when(is_leaf)
+    def _():
+        pl.semaphore_signal(barrier, inc=1, device_id=(hub_of[0], my_kv), device_id_type=MESH)
 
     def remote(src, dst, send, recv, target):
         return pltpu.make_async_remote_copy(
@@ -94,32 +97,52 @@
         if count:
             pltpu.make_async_copy(buffer.at[pl.ds(0, count)], buffer.at[pl.ds(0, count)], sem).wait()
 
+    small[1].wait()
+    for h in range(HQ):
+        q_rows[h : h + 1, :] = q_ref[0:1, h * HEAD_SIZE : (h + 1) * HEAD_SIZE].astype(jnp.float32)
+    q_own[...] = q_rows[...].astype(jnp.bfloat16)
     small[0].wait()
     lane1 = lax.broadcasted_iota(jnp.int32, (1, HEAD_SIZE), 1)
     own_table = jnp.full((1, HEAD_SIZE), -1.0, jnp.float32)
     for s in range(slots):
         own_table = jnp.where(lane1 == s, owner_ref[s].astype(jnp.float32), own_table)
     table[my_req] = own_table
-    small[1].wait()
-    for h in range(HQ):
-        q_rows[h : h + 1, :] = q_ref[0:1, h * HEAD_SIZE : (h + 1) * HEAD_SIZE].astype(jnp.float32)
-    own_query = q_rows[...].astype(jnp.bfloat16)
-    q_own[...] = own_query
-    small[2].wait()
-    small[3].wait()
-
-    pl.semaphore_wait(barrier, n_kv + n_chip - 1 - core)
 
     mine = core * n_kv + my_kv
-    for d in range(n_chip - 1, 0, -1):
-        remote(table.at[my_req], table.at[my_req], ts_sem.at[0], tr_sem.at[0], (hub_of[d], my_kv)).start()
-    for d in range(n_kv - 1, 0, -1):
-        remote(q_own, q_col.at[mine], qs_sem.at[0], qr_sem.at[0], (hub_of[0], kv_peers[d])).start()
+
+    def send_query():
+        for d in range(n_kv - 1, 0, -1):
+            remote(q_own, q_col.at[mine], qs_sem.at[0], qr_sem.at[0], (hub_of[0], kv_peers[d])).start()
+
+    def send_table():
+        for d in range(n_chip - 1, 0, -1):
+            remote(table.at[my_req], table.at[my_req], ts_sem.at[0], tr_sem.at[d], (hub_of[d], my_kv)).start()
 
     @pl.when(is_leaf)
     def _():
+        pl.semaphore_wait(barrier, n_kv)
+        pl.semaphore_signal(met_sem, inc=1, device_id=(hub_of[0], my_kv), device_id_type=MESH)
+        send_query()
+        remote(q_own, q_col.at[mine], qs_sem.at[0], qr_sem.at[0], (hub_of[0], my_kv)).start()
         remote(table.at[my_req], table.at[my_req], ts_sem.at[0], tr_sem.at[0], (hub_of[0], my_kv)).start()
-        remote(q_own, q_col.at[mine], qs_sem.at[0], qr_sem.at[0], (hub_of[0], my_kv)).start()
+        pl.semaphore_wait(met_sem, 1)
+        send_table()
+
+    @pl.when(is_hub)
+    def _():
+        pl.semaphore_wait(barrier, n_chip)
+        pl.semaphore_signal(met_sem, inc=1, device_id=(leaf_of[0], my_kv), device_id_type=MESH)
+        send_table()
+        pl.semaphore_wait(met_sem, 1)
+        send_query()
+
+    for copy in small[2:]:
+        copy.start()
+    for s in range(slots):
+        pltpu.make_async_copy(key_hbm.at[s], keys.at[s], page_sem.at[0]).start()
+        pltpu.make_async_copy(value_hbm.at[s], values.at[s], page_sem.at[1]).start()
+    for copy in small[2:]:
+        copy.wait()
 
     homes = []
     for d in range(n_chip):
@@ -127,36 +150,36 @@
         for b in range(CORES):
             index, present = jnp.int32(0), jnp.int32(0)
             for s in range(slots):
-                same = lax.div(owner_ref[s], group) == leaf_of[d] + b
+                same = lax.div(owner_ref[s], group) == d * CORES + b
                 index = jnp.where(same, jnp.int32(s), index)
                 present = jnp.where(same, jnp.int32(1), present)
             limit = length_ref[owner_ref[index]] - number_ref[index] * page_tokens
-            pair.append((index, limit * present))
+            place = jnp.where(present == 1, owner_ref[index] - (d * CORES + b) * group, -1)
+            pair.append((index, limit * present, place))
         homes.append(pair)
 
     edges = [0, max(n_chip // 4, 1), max(3 * n_chip // 4, 1), n_chip]
-    stage_of = [sum(d >= edge for edge in edges[1:]) for d in range(n_chip)]
+    alone = [jnp.logical_and(is_hub, my_chip == c) for c in range(n_chip)]
+    met = [jnp.logical_not(own) for own in alone]
 
     @pl.when(is_hub)
     def _():
         q_col[(CORES - 1) * n_kv + my_kv] = q_own[...]
-        arrived(table, n_req - 1, tr_sem.at[0])
-        picks = {}
-        for d in range(n_chip - 1, -1, -1):
+        arrived(q_col, CORES * n_kv - 1, qr_sem.at[0])
+        choices = [q_col[c].astype(jnp.float32) for c in range(CORES * group)]
+        for d in range(n_chip):
+            arrived(table, CORES if d else CORES - 1, tr_sem.at[d])
+            picks = {}
             for a in range(CORES):
                 row = table[leaf_of[d] + a]
                 for b in range(CORES):
                     rel = row - ((leaf_of[0] + b) * group).astype(jnp.float32)
                     inside = jnp.logical_and(rel >= 0.0, rel < float(group))
-                    picks[d, a, b] = jnp.max(jnp.where(inside, rel, -1.0), axis=1, keepdims=True)
-        for (d, a, b), pick in picks.items():
-            held[b, d * CORES + a] = jnp.broadcast_to(pick, (1, HEAD_SIZE))
-        arrived(q_col, CORES * n_kv - 1, qr_sem.at[0])
-        choices = [q_col[c].astype(jnp.float32) for c in range(CORES * group)]
-        for d in range(n_chip - 1, -1, -1):
+                    picks[a, b] = jnp.max(jnp.where(inside, rel, -1.0), axis=1, keepdims=True)
             for a in range(CORES):
                 for b in range(CORES):
-                    pick = jnp.broadcast_to(picks[d, a, b], (HQ, HEAD_SIZE))
+                    held[b, leaf_of[d] + a] = jnp.broadcast_to(picks[a, b], (1, HEAD_SIZE))
+                    pick = jnp.broadcast_to(picks[a, b], (HQ, HEAD_SIZE))
                     chosen = jnp.zeros((HQ, HEAD_SIZE), jnp.float32)
                     for c in range(group):
                         chosen = jnp.where(pick == float(c), choices[b * group + c], chosen)
@@ -166,7 +189,7 @@
                         q_send[d * CORES + a, b] = chosen.astype(jnp.bfloat16)
                 if d or a < CORES - 1:
                     remote(
-                        q_send.at[d * CORES + a], q_in.at[my_chip], ds_sem.at[0], dr_sem.at[stage_of[d]],
+                        q_send.at[d * CORES + a], q_in.at[my_chip], ds_sem.at[0], dr_sem.at[my_chip],
                         (leaf_of[d] + a, my_kv),
                     ).start()
 
@@ -181,18 +204,17 @@
     wide = 2 * HEAD_SIZE
 
     for stage, (low, high) in enumerate(zip(edges[:-1], edges[1:])):
-        batch = [(d, b) for d in range(high - 1, low - 1, -1) for b in range(CORES)]
-        if low == 0:
-
-            @pl.when(is_leaf)
+        batch = [(c, b) for c in range(low, high) for b in range(CORES)]
+        for c in range(low, high):
+
+            @pl.when(met[c])
             def _():
-                arrived(q_in, 1, dr_sem.at[0])
-
-        arrived(q_in, high - max(low, 1), dr_sem.at[stage])
+                arrived(q_in, 1, dr_sem.at[c])
+
         scored = {}
         for d, b in batch:
-            index, limit = homes[d][b]
-            query = q_in[chip_peers[d], b].astype(jnp.float32)
+            index, limit, _ = homes[d][b]
+            query = q_in[d, b].astype(jnp.float32)
             pieces = []
             for k in range(HQ // PAIR):
                 q8 = query[k * PAIR : (k + 1) * PAIR]
@@ -210,8 +232,9 @@
         tops = {e: jnp.max(scored[e], axis=1, keepdims=True) for e in batch}
         weights = {e: jnp.exp(scored[e] - tops[e]) for e in batch}
         totals = {e: jnp.sum(weights[e], axis=1, keepdims=True) for e in batch}
+        summed, largest = {}, {}
         for d, b in batch:
-            index, limit = homes[d][b]
+            index, _, _ = homes[d][b]
             blocks = []
             for k in range(HQ // PAIR):
                 w8 = weights[d, b][k * PAIR : (k + 1) * PAIR].astype(jnp.bfloat16)
@@ -219,30 +242,50 @@
                     w8, values[index, :, k * wide : (k + 1) * wide], preferred_element_type=jnp.float32
                 )
                 blocks.append(jnp.where(first, both[:, :HEAD_SIZE], both[:, HEAD_SIZE:]))
-            blocks.append(diagonal_to_lanes(tops[d, b], on_diagonal))
-            blocks.append(diagonal_to_lanes(totals[d, b], on_diagonal))
-            part_send[d, b] = jnp.concatenate(blocks, axis=0)
+            blocks = jnp.concatenate(blocks, axis=0)
+            largest[d, b] = jnp.maximum(jnp.max(jnp.abs(blocks), axis=1, keepdims=True), finest)
+            summed[d, b] = blocks
+        for d, b in batch:
+            coded = jnp.round(summed[d, b] * (STEPS / largest[d, b]))
+            part_send[d, b] = coded.astype(jnp.int32).astype(jnp.int16)
+            lanes = [diagonal_to_lanes(column[d, b], on_diagonal) for column in (tops, totals, largest)]
+            stat_send[d, b] = jnp.concatenate(lanes, axis=0)
+            if d < n_near:
+                lanes[0] = jnp.where(homes[d][b][2] == 0, lanes[0], lowest)
+                near_send[d, b] = jnp.concatenate(lanes, axis=0)
             if b < CORES - 1:
                 continue
-            copy = remote(part_send.at[d], part_in.at[my_req], ps_sem.at[0], pr_sem.at[0], (hub_of[d], my_kv))
-            if d == 0:
-                pl.when(is_leaf)(copy.start)
-            else:
+            target = (d * CORES + CORES - 1, my_kv)
+            copy = remote(part_send.at[d], part_in.at[my_req], ps_sem.at[0], pr_sem.at[0], target)
+            stat_copy = remote(stat_send.at[d], stat_in.at[my_req], ss_sem.at[0], sr_sem.at[0], target)
+
+            if d < n_near:
+
+                @pl.when(is_last)
+                def _():
+                    for a in range(CORES):
+                        owner = (d * CORES + a, 0)
+                        remote(near_send.at[d, a], near_stat.at[my_req], ns_sem.at[0], nr_sem.at[0], owner).start()
+                        remote(part_send.at[d, a], near_in.at[my_req], ns_sem.at[1], nr_sem.at[1], owner).start()
+
+            @pl.when(met[d])
+            def _():
+                stat_copy.start()
                 copy.start()
 
+
     @pl.when(is_hub)
     def _():
+        part_in[my_req] = part_send[my_chip]
+        stat_in[my_req] = stat_send[my_chip]
+        arrived(stat_in, n_req - 1, sr_sem.at[0])
         arrived(part_in, n_req - 1, pr_sem.at[0])
         for b in range(CORES):
-            sources = []
-            for d in range(n_chip):
-                for a in range(CORES):
-                    if d == 0 and a == CORES - 1:
-                        sources.append(part_send.at[0, b])
-                    else:
-                        sources.append(part_in.at[leaf_of[d] + a, b])
-            tops = [source[HQ : HQ + 1, :] for source in sources]
-            totals = [source[HQ + 1 : HQ + 2, :] for source in sources]
+            sources = [part_in.at[e, b] for e in range(n_req)]
+            stats = [stat_in.at[e, b] for e in range(n_req)]
+            tops = [stat[0:1, :] for stat in stats]
+            totals = [stat[1:2, :] for stat in stats]
+            steps = [stat[2:3, :] * (1.0 / STEPS) for stat in stats]
             picks = [held[b, e] for e in range(n_req)]
             member = [[picks[e] == float(c) for e in range(n_req)] for c in range(group)]
             merged_top, merged_total = [], []
@@ -264,7 +307,8 @@
                 merged_total.append(amount)
             sums = [jnp.zeros((HQ, HEAD_SIZE), jnp.float32) for _ in range(group)]
             for e in range(n_req):
-                scaled = lanes_to_column(factors[e], on_diagonal) * sources[e][0:HQ, :]
+                coded = sources[e][...].astype(jnp.int32).astype(jnp.float32)
+                scaled = lanes_to_column(factors[e] * steps[e], on_diagonal) * coded
                 pick = jnp.broadcast_to(picks[e], (HQ, HEAD_SIZE))
                 for c in range(group):
                     sums[c] = sums[c] + jnp.where(pick == float(c), scaled, 0.0)
@@ -275,18 +319,44 @@
                 if d == 0 and b == CORES - 1:
                     merged_in[my_kv] = merged[b * n_kv + my_kv]
                     continue
-                remote(
+                copy = remote(
                     merged.at[b * n_kv + kv_peers[d]], merged_in.at[my_kv], ms_sem.at[0], mr_sem.at[0],
                     (leaf_of[0] + b, kv_peers[d]),
-                ).start()
-
-    @pl.when(is_leaf)
-    def _():
-        arrived(merged_in, n_kv, mr_sem.at[0])
-
-    @pl.when(is_hub)
-    def _():
-        arrived(merged_in, n_kv - 1, mr_sem.at[0])
+                )
+                if d == 0:
+                    copy.start()
+                else:
+                    skipped = jnp.logical_and(jnp.logical_and(is_last, kv_peers[d] == 0), my_chip < n_near)
+                    pl.when(jnp.logical_not(skipped))(copy.start)
+
+    for role, others in ((is_leaf, n_kv), (is_hub, n_kv - 1)):
+
+        @pl.when(jnp.logical_and(role, jnp.logical_not(is_near)))
+        def _():
+            arrived(merged_in, others, mr_sem.at[0])
+
+        @pl.when(jnp.logical_and(role, is_near))
+        def _():
+            arrived(merged_in, others - 1, mr_sem.at[0])
+
+    @pl.when(is_near)
+    def _():
+        arrived(near_stat, n_req, nr_sem.at[0])
+        tops = [near_stat[e, 0:1, :] for e in range(n_req)]
+        best = tops[0]
+        for e in range(1, n_req):
+            best = jnp.maximum(best, tops[e])
+        factors = [jnp.exp(tops[e] - best) for e in range(n_req)]
+        amount = jnp.zeros((1, HEAD_SIZE), jnp.float32)
+        for e in range(n_req):
+            amount = amount + factors[e] * near_stat[e, 1:2, :]
+        arrived(near_in, n_req, nr_sem.at[1])
+        total = jnp.zeros((HQ, HEAD_SIZE), jnp.float32)
+        for e in range(n_req):
+            step = factors[e] * (near_stat[e, 2:3, :] * (1.0 / STEPS))
+            total = total + lanes_to_column(step, on_diagonal) * near_in[e].astype(jnp.int32).astype(jnp.float32)
+        merged_in[n_kv - 1, 0:HQ, :] = total
+        merged_in[n_kv - 1, HQ : HQ + 2, :] = jnp.concatenate([best, amount], axis=0)
 
     tops = [merged_in[c, HQ : HQ + 1, :] for c in range(n_kv)]
     best = tops[0]
@@ -307,14 +377,30 @@
         arrived(q_col, n_kv, qs_sem.at[0])
         arrived(table, n_chip, ts_sem.at[0])
         arrived(part_send, n_chip, ps_sem.at[0])
+        arrived(stat_send, n_chip, ss_sem.at[0])
 
     @pl.when(is_hub)
     def _():
         arrived(q_col, n_kv - 1, qs_sem.at[0])
         arrived(table, n_chip - 1, ts_sem.at[0])
         arrived(part_send, n_chip - 1, ps_sem.at[0])
+        arrived(stat_send, n_chip - 1, ss_sem.at[0])
         arrived(q_send, n_req - 1, ds_sem.at[0])
+
+    sends_near = jnp.logical_and(is_last, my_chip < n_near)
+
+    @pl.when(jnp.logical_and(is_hub, jnp.logical_not(sends_near)))
+    def _():
         arrived(merged, CORES * n_kv - 1, ms_sem.at[0])
+
+    @pl.when(jnp.logical_and(is_hub, sends_near))
+    def _():
+        arrived(merged, CORES * n_kv - 1 - CORES, ms_sem.at[0])
+
+    @pl.when(is_last)
+    def _():
+        arrived(near_send, n_near, ns_sem.at[0])
+        arrived(part_send, n_near, ns_sem.at[1])
 
 
 def solution(mesh):
@@ -347,16 +433,24 @@
                 pltpu.VMEM((CORES, n_req, 1, HEAD_SIZE), jnp.float32),
                 pltpu.VMEM((n_req, CORES, HQ, HEAD_SIZE), jnp.bfloat16),
                 pltpu.VMEM((n_chip, CORES, HQ, HEAD_SIZE), jnp.bfloat16),
-                pltpu.VMEM((n_chip, CORES) + blob, jnp.float32),
-                pltpu.VMEM((n_req, CORES) + blob, jnp.float32),
+                pltpu.VMEM((n_chip, CORES, HQ, HEAD_SIZE), jnp.int16),
+                pltpu.VMEM((n_req, CORES, HQ, HEAD_SIZE), jnp.int16),
+                pltpu.VMEM((n_chip, CORES, 3, HEAD_SIZE), jnp.float32),
+                pltpu.VMEM((n_req, CORES, 3, HEAD_SIZE), jnp.float32),
+                pltpu.VMEM((n_chip, CORES, 3, HEAD_SIZE), jnp.float32),
+                pltpu.VMEM((n_req, HQ, HEAD_SIZE), jnp.int16),
+                pltpu.VMEM((n_req, 3, HEAD_SIZE), jnp.float32),
                 pltpu.VMEM((CORES * n_kv,) + blob, jnp.float32),
                 pltpu.VMEM((n_kv,) + blob, jnp.float32),
+                pltpu.SemaphoreType.REGULAR,
                 dma((4,)),
                 dma((2,)),
                 dma((1,)), dma((1,)),
+                dma((1,)), dma((n_chip,)),
+                dma((1,)), dma((n_chip,)),
                 dma((1,)), dma((1,)),
-                dma((1,)), dma((3,)),
                 dma((1,)), dma((1,)),
+                dma((2,)), dma((2,)),
                 dma((1,)), dma((1,)),
             ],
             compiler_params=pltpu.CompilerParams(collective_id=0, has_side_effects=True),

time: 19.5 us -> 18.7 us (0.959)
  Pallas kernels: 18.7 us -> 17.8 us
    pallas_call x1, Pallas kernels: 18.7 us -> 17.8 us  [on_device(): pl.pallas_call(functools.partial(kernel, n_req, n_kv, group), out_shape=p...]
where the time goes in v2:
time: 18.7 us; the launch traced here: 18.5 us
  Pallas kernels  17.8 us (95%)
  local copies, waits for them, and re-layouts  0.62 us (3%)
    pallas_call x1, Pallas kernels, on_device(): pl.pallas_call(functools.partial(kernel, n_req, n_kv, group), out_shape=p...  17.8 us
    unnamed x1, local copies, waits for them, and re-layouts  0.62 us

profile of v2, /device:TPU:0, one launch (start us, length us, event | category | flops | bytes accessed | tf_op | source)
XLA Modules:
  0.0 18.5 jit_solution(15461986001113505271)
XLA Ops:
  0.0 17.8 %shard_map.64 = bf16[32,128]{1,0:T(8,128)(2,1)S(1)} custom-call(s32[6]{0:T(128)} %owner_hbm.1, s32[6]{0:T(128)} %number_hbm.1, s32[32]{0:T(128)} %length_hbm.1, bf16[1,4096]{1,0:T(2,128)(2,1)} %q_hbm.1, bf16[6,128,1024]{2,1,0:T(8,128)(2,1)} %key_hbm.1, bf16[6,128,1024]{2,1,0:T(8,128)(2,1)} %value_hbm.1), custom_call_target="tpu_custom_call" | custom-call | tf_op jit(solution)/shard_map/pallas_call | solution.py:417
  17.8 0.6 %copy.9 = bf16[1,1,32,128]{3,1,2,0:T(2,128)(2,1)} copy(bf16[1,1,32,128]{3,2,1,0:T(8,128)(2,1)S(1)} %bitcast.5) | data formatting | bytes 16384

commit v3 on v2

--- a/solution.py
+++ b/solution.py
@@ -47,7 +47,7 @@
     owner_hbm, number_hbm, length_hbm, q_hbm, key_hbm, value_hbm, out_ref,
     owner_ref, number_ref, length_ref, q_ref, keys, values, q_rows, q_own, q_col, table, held, q_send, q_in,
     part_send, part_in, stat_send, stat_in, near_send, near_in, near_stat, merged, merged_in,
-    met_sem, small_sem, page_sem, qs_sem, qr_sem, ts_sem, tr_sem, ds_sem, dr_sem, ps_sem, pr_sem, ss_sem, sr_sem, ns_sem, nr_sem, ms_sem, mr_sem,
+    met_sem, far_sem, small_sem, page_sem, qs_sem, qr_sem, ts_sem, tr_sem, ds_sem, dr_sem, ps_sem, pr_sem, ss_sem, sr_sem, ns_sem, nr_sem, ms_sem, mr_sem,
 ):
     slots, page_tokens, _ = keys.shape
     n_chip = n_req // CORES
@@ -59,6 +59,8 @@
     is_hub = core == CORES - 1
     is_leaf = core < CORES - 1
     is_last = my_kv == n_kv - 1
+    is_relay = my_kv == n_kv - 2
+    is_early = my_kv < n_kv - 2
     is_near = jnp.logical_and(my_kv == 0, my_chip < n_near)
     chip_peers = partners(my_chip, n_chip)
     kv_peers = partners(my_kv, n_kv)
@@ -78,8 +80,12 @@
 
     @pl.when(is_hub)
     def _():
-        for d in range(n_kv - 1, -1, -1):
-            pl.semaphore_signal(barrier, inc=1, device_id=(leaf_of[0], kv_peers[d]), device_id_type=MESH)
+        for z in range(n_kv - 1, -1, -1):
+
+            @pl.when(jnp.logical_not(jnp.logical_and(is_last, z < n_kv - 2)))
+            def _():
+                pl.semaphore_signal(barrier, inc=1, device_id=(leaf_of[0], z), device_id_type=MESH)
+
         for d in range(n_chip - 1, 0, -1):
             pl.semaphore_signal(barrier, inc=1, device_id=(hub_of[d], my_kv), device_id_type=MESH)
 
@@ -110,31 +116,59 @@
 
     mine = core * n_kv + my_kv
 
-    def send_query():
-        for d in range(n_kv - 1, 0, -1):
-            remote(q_own, q_col.at[mine], qs_sem.at[0], qr_sem.at[0], (hub_of[0], kv_peers[d])).start()
+    def send_query(last):
+        for z in range(last, -1, -1):
+
+            @pl.when(my_kv != z)
+            def _():
+                remote(q_own, q_col.at[mine], qs_sem.at[0], qr_sem.at[0], (hub_of[0], z)).start()
 
     def send_table():
         for d in range(n_chip - 1, 0, -1):
             remote(table.at[my_req], table.at[my_req], ts_sem.at[0], tr_sem.at[d], (hub_of[d], my_kv)).start()
 
-    @pl.when(is_leaf)
-    def _():
-        pl.semaphore_wait(barrier, n_kv)
+    def leaf_column(early):
+        pl.semaphore_wait(barrier, n_kv - 1 if early else n_kv)
         pl.semaphore_signal(met_sem, inc=1, device_id=(hub_of[0], my_kv), device_id_type=MESH)
-        send_query()
-        remote(q_own, q_col.at[mine], qs_sem.at[0], qr_sem.at[0], (hub_of[0], my_kv)).start()
-        remote(table.at[my_req], table.at[my_req], ts_sem.at[0], tr_sem.at[0], (hub_of[0], my_kv)).start()
+        remote(q_own, q_col.at[mine], qs_sem.at[0], qr_sem.at[1], (hub_of[0], my_kv)).start()
+        send_query(n_kv - 2 if early else n_kv - 1)
+
+        @pl.when(is_relay)
+        def _():
+            for z in range(n_kv - 2):
+                pl.semaphore_signal(far_sem, inc=1, device_id=(hub_of[0], z), device_id_type=MESH)
+
+    def leaf_plane():
         pl.semaphore_wait(met_sem, 1)
         send_table()
-
-    @pl.when(is_hub)
-    def _():
+        remote(table.at[my_req], table.at[my_req], ts_sem.at[0], tr_sem.at[0], (hub_of[0], my_kv)).start()
+
+    def hub_column(early):
+        pl.semaphore_wait(met_sem, 1)
+        send_query(n_kv - 2 if early else n_kv - 1)
+        if early:
+            arrived(q_col, 1, qr_sem.at[1])
+            pl.semaphore_wait(far_sem, 1)
+            last = (hub_of[0], n_kv - 1)
+            remote(q_own, q_col.at[mine], qs_sem.at[0], qr_sem.at[0], last).start()
+            remote(q_col.at[my_kv], q_col.at[my_kv], qs_sem.at[0], qr_sem.at[0], last).start()
+
+    def hub_plane():
         pl.semaphore_wait(barrier, n_chip)
         pl.semaphore_signal(met_sem, inc=1, device_id=(leaf_of[0], my_kv), device_id_type=MESH)
         send_table()
-        pl.semaphore_wait(met_sem, 1)
-        send_query()
+
+    for role, column, plane in ((is_leaf, leaf_column, leaf_plane), (is_hub, hub_column, hub_plane)):
+
+        @pl.when(jnp.logical_and(role, jnp.logical_not(is_early)))
+        def _():
+            column(False)
+            plane()
+
+        @pl.when(jnp.logical_and(role, is_early))
+        def _():
+            plane()
+            column(True)
 
     for copy in small[2:]:
         copy.start()
@@ -165,9 +199,14 @@
     @pl.when(is_hub)
     def _():
         q_col[(CORES - 1) * n_kv + my_kv] = q_own[...]
-        arrived(q_col, CORES * n_kv - 1, qr_sem.at[0])
+        arrived(q_col, CORES * n_kv - 2, qr_sem.at[0])
+
+        @pl.when(jnp.logical_not(is_early))
+        def _():
+            arrived(q_col, 1, qr_sem.at[1])
+
         choices = [q_col[c].astype(jnp.float32) for c in range(CORES * group)]
-        for d in range(n_chip):
+        for d in range(n_chip - 1, -1, -1):
             arrived(table, CORES if d else CORES - 1, tr_sem.at[d])
             picks = {}
             for a in range(CORES):
@@ -274,6 +313,17 @@
                 copy.start()
 
 
+    def send_merged(b, z):
+        skipped = is_last if z == 0 and n_near == n_chip else jnp.bool_(False)
+        if b == CORES - 1:
+            skipped = jnp.logical_or(skipped, my_kv == z)
+
+        @pl.when(jnp.logical_not(skipped))
+        def _():
+            remote(
+                merged.at[b * n_kv + z], merged_in.at[my_kv], ms_sem.at[0], mr_sem.at[0], (leaf_of[0] + b, z)
+            ).start()
+
     @pl.when(is_hub)
     def _():
         part_in[my_req] = part_send[my_chip]
@@ -315,19 +365,12 @@
             for c in range(group):
                 merged[b * n_kv + c, 0:HQ, :] = sums[c]
                 merged[b * n_kv + c, HQ : HQ + 2, :] = jnp.concatenate([merged_top[c], merged_total[c]], axis=0)
-            for d in range(n_kv - 1, -1, -1):
-                if d == 0 and b == CORES - 1:
-                    merged_in[my_kv] = merged[b * n_kv + my_kv]
-                    continue
-                copy = remote(
-                    merged.at[b * n_kv + kv_peers[d]], merged_in.at[my_kv], ms_sem.at[0], mr_sem.at[0],
-                    (leaf_of[0] + b, kv_peers[d]),
-                )
-                if d == 0:
-                    copy.start()
-                else:
-                    skipped = jnp.logical_and(jnp.logical_and(is_last, kv_peers[d] == 0), my_chip < n_near)
-                    pl.when(jnp.logical_not(skipped))(copy.start)
+            send_merged(b, 0)
+
+        for z in range(1, n_kv):
+            for b in range(CORES):
+                send_merged(b, z)
+        merged_in[my_kv] = merged[(CORES - 1) * n_kv + my_kv]
 
     for role, others in ((is_leaf, n_kv), (is_hub, n_kv - 1)):
 
@@ -372,16 +415,25 @@
     result = result / lanes_to_column(amount, on_diagonal)
     out_ref[...] = result.astype(jnp.bfloat16)
 
+    for early, leaf_sent, hub_sent in ((True, n_kv - 1, n_kv), (False, n_kv, n_kv - 1)):
+        now = is_early if early else jnp.logical_not(is_early)
+
+        @pl.when(jnp.logical_and(is_leaf, now))
+        def _():
+            arrived(q_col, leaf_sent, qs_sem.at[0])
+
+        @pl.when(jnp.logical_and(is_hub, now))
+        def _():
+            arrived(q_col, hub_sent, qs_sem.at[0])
+
     @pl.when(is_leaf)
     def _():
-        arrived(q_col, n_kv, qs_sem.at[0])
         arrived(table, n_chip, ts_sem.at[0])
         arrived(part_send, n_chip, ps_sem.at[0])
         arrived(stat_send, n_chip, ss_sem.at[0])
 
     @pl.when(is_hub)
     def _():
-        arrived(q_col, n_kv - 1, qs_sem.at[0])
         arrived(table, n_chip - 1, ts_sem.at[0])
         arrived(part_send, n_chip - 1, ps_sem.at[0])
         arrived(stat_send, n_chip - 1, ss_sem.at[0])
@@ -443,9 +495,10 @@
                 pltpu.VMEM((CORES * n_kv,) + blob, jnp.float32),
                 pltpu.VMEM((n_kv,) + blob, jnp.float32),
                 pltpu.SemaphoreType.REGULAR,
+                pltpu.SemaphoreType.REGULAR,
                 dma((4,)),
                 dma((2,)),
-                dma((1,)), dma((1,)),
+                dma((1,)), dma((2,)),
                 dma((1,)), dma((n_chip,)),
                 dma((1,)), dma((n_chip,)),
                 dma((1,)), dma((1,)),

time: 18.7 us -> 18.2 us (0.973)
  Pallas kernels: 17.8 us -> 17.4 us
    pallas_call x1, Pallas kernels: 17.8 us -> 17.4 us  [on_device(): pl.pallas_call(functools.partial(kernel, n_req, n_kv, group), out_shape=p...]
where the time goes in v3:
time: 18.2 us; the launch traced here: 18 us
  Pallas kernels  17.4 us (96%)
  local copies, waits for them, and re-layouts  0.62 us (3%)
    pallas_call x1, Pallas kernels, on_device(): pl.pallas_call(functools.partial(kernel, n_req, n_kv, group), out_shape=p...  17.4 us
    unnamed x1, local copies, waits for them, and re-layouts  0.62 us

profile of v3, /device:TPU:0, one launch (start us, length us, event | category | flops | bytes accessed | tf_op | source)
XLA Modules:
  0.0 18.0 jit_solution(4528761469944206346)
XLA Ops:
  0.0 17.4 %shard_map.64 = bf16[32,128]{1,0:T(8,128)(2,1)S(1)} custom-call(s32[6]{0:T(128)} %owner_hbm.1, s32[6]{0:T(128)} %number_hbm.1, s32[32]{0:T(128)} %length_hbm.1, bf16[1,4096]{1,0:T(2,128)(2,1)} %q_hbm.1, bf16[6,128,1024]{2,1,0:T(8,128)(2,1)} %key_hbm.1, bf16[6,128,1024]{2,1,0:T(8,128)(2,1)} %value_hbm.1), custom_call_target="tpu_custom_call" | custom-call | tf_op jit(solution)/shard_map/pallas_call | solution.py:469
  17.4 0.6 %copy.9 = bf16[1,1,32,128]{3,1,2,0:T(2,128)(2,1)} copy(bf16[1,1,32,128]{3,2,1,0:T(8,128)(2,1)S(1)} %bitcast.5) | data formatting | bytes 16384

commit v4 on v3

--- a/solution.py
+++ b/solution.py
@@ -51,7 +51,7 @@
 ):
     slots, page_tokens, _ = keys.shape
     n_chip = n_req // CORES
-    n_near = n_chip
+    n_second = max(3 * n_chip // 4, 1)
     my_req = lax.axis_index("req")
     my_kv = lax.axis_index("kv")
     my_chip = lax.div(my_req, CORES)
@@ -61,7 +61,8 @@
     is_last = my_kv == n_kv - 1
     is_relay = my_kv == n_kv - 2
     is_early = my_kv < n_kv - 2
-    is_near = jnp.logical_and(my_kv == 0, my_chip < n_near)
+    is_near = my_kv == 0
+    is_nearest = jnp.logical_and(my_kv == 0, my_chip < n_second)
     chip_peers = partners(my_chip, n_chip)
     kv_peers = partners(my_kv, n_kv)
     hub_of = [CORES * chip + CORES - 1 for chip in chip_peers]
@@ -289,23 +290,24 @@
             part_send[d, b] = coded.astype(jnp.int32).astype(jnp.int16)
             lanes = [diagonal_to_lanes(column[d, b], on_diagonal) for column in (tops, totals, largest)]
             stat_send[d, b] = jnp.concatenate(lanes, axis=0)
-            if d < n_near:
-                lanes[0] = jnp.where(homes[d][b][2] == 0, lanes[0], lowest)
-                near_send[d, b] = jnp.concatenate(lanes, axis=0)
+            lanes[0] = jnp.where(homes[d][b][2] == 0, lanes[0], lowest)
+            near_send[d, b] = jnp.concatenate(lanes, axis=0)
             if b < CORES - 1:
                 continue
             target = (d * CORES + CORES - 1, my_kv)
             copy = remote(part_send.at[d], part_in.at[my_req], ps_sem.at[0], pr_sem.at[0], target)
             stat_copy = remote(stat_send.at[d], stat_in.at[my_req], ss_sem.at[0], sr_sem.at[0], target)
 
-            if d < n_near:
-
-                @pl.when(is_last)
+            for plane, chips in enumerate((n_chip, n_second)):
+                if d >= chips:
+                    continue
+
+                @pl.when(my_kv == n_kv - 1 - plane)
                 def _():
                     for a in range(CORES):
-                        owner = (d * CORES + a, 0)
-                        remote(near_send.at[d, a], near_stat.at[my_req], ns_sem.at[0], nr_sem.at[0], owner).start()
-                        remote(part_send.at[d, a], near_in.at[my_req], ns_sem.at[1], nr_sem.at[1], owner).start()
+                        owner, e, k = (d * CORES + a, 0), plane * n_req + my_req, 2 * plane
+                        remote(near_send.at[d, a], near_stat.at[e], ns_sem.at[k], nr_sem.at[k], owner).start()
+                        remote(part_send.at[d, a], near_in.at[e], ns_sem.at[k + 1], nr_sem.at[k + 1], owner).start()
 
             @pl.when(met[d])
             def _():
@@ -313,8 +315,10 @@
                 copy.start()
 
 
+    sends_near = jnp.logical_or(is_last, jnp.logical_and(is_relay, my_chip < n_second))
+
     def send_merged(b, z):
-        skipped = is_last if z == 0 and n_near == n_chip else jnp.bool_(False)
+        skipped = sends_near if z == 0 else jnp.bool_(False)
         if b == CORES - 1:
             skipped = jnp.logical_or(skipped, my_kv == z)
 
@@ -378,28 +382,38 @@
         def _():
             arrived(merged_in, others, mr_sem.at[0])
 
-        @pl.when(jnp.logical_and(role, is_near))
+        @pl.when(jnp.logical_and(role, jnp.logical_and(is_near, jnp.logical_not(is_nearest))))
         def _():
             arrived(merged_in, others - 1, mr_sem.at[0])
 
-    @pl.when(is_near)
-    def _():
-        arrived(near_stat, n_req, nr_sem.at[0])
-        tops = [near_stat[e, 0:1, :] for e in range(n_req)]
-        best = tops[0]
-        for e in range(1, n_req):
-            best = jnp.maximum(best, tops[e])
-        factors = [jnp.exp(tops[e] - best) for e in range(n_req)]
+        @pl.when(jnp.logical_and(role, is_nearest))
+        def _():
+            arrived(merged_in, others - 2, mr_sem.at[0])
+
+    def merge_near(plane):
+        arrived(near_stat, n_req, nr_sem.at[2 * plane])
+        some = range(plane * n_req, (plane + 1) * n_req)
+        tops = {e: near_stat[e, 0:1, :] for e in some}
+        best = functools.reduce(jnp.maximum, tops.values())
+        factors = {e: jnp.exp(tops[e] - best) for e in some}
         amount = jnp.zeros((1, HEAD_SIZE), jnp.float32)
-        for e in range(n_req):
+        for e in some:
             amount = amount + factors[e] * near_stat[e, 1:2, :]
-        arrived(near_in, n_req, nr_sem.at[1])
+        arrived(near_in, n_req, nr_sem.at[2 * plane + 1])
         total = jnp.zeros((HQ, HEAD_SIZE), jnp.float32)
-        for e in range(n_req):
+        for e in some:
             step = factors[e] * (near_stat[e, 2:3, :] * (1.0 / STEPS))
             total = total + lanes_to_column(step, on_diagonal) * near_in[e].astype(jnp.int32).astype(jnp.float32)
-        merged_in[n_kv - 1, 0:HQ, :] = total
-        merged_in[n_kv - 1, HQ : HQ + 2, :] = jnp.concatenate([best, amount], axis=0)
+        merged_in[n_kv - 1 - plane, 0:HQ, :] = total
+        merged_in[n_kv - 1 - plane, HQ : HQ + 2, :] = jnp.concatenate([best, amount], axis=0)
+
+    @pl.when(is_nearest)
+    def _():
+        merge_near(1)
+
+    @pl.when(is_near)
+    def _():
+        merge_near(0)
 
     tops = [merged_in[c, HQ : HQ + 1, :] for c in range(n_kv)]
     best = tops[0]
@@ -439,8 +453,6 @@
         arrived(stat_send, n_chip - 1, ss_sem.at[0])
         arrived(q_send, n_req - 1, ds_sem.at[0])
 
-    sends_near = jnp.logical_and(is_last, my_chip < n_near)
-
     @pl.when(jnp.logical_and(is_hub, jnp.logical_not(sends_near)))
     def _():
         arrived(merged, CORES * n_kv - 1, ms_sem.at[0])
@@ -449,10 +461,12 @@
     def _():
         arrived(merged, CORES * n_kv - 1 - CORES, ms_sem.at[0])
 
-    @pl.when(is_last)
-    def _():
-        arrived(near_send, n_near, ns_sem.at[0])
-        arrived(part_send, n_near, ns_sem.at[1])
+    for plane, chips in enumerate((n_chip, n_second)):
+
+        @pl.when(my_kv == n_kv - 1 - plane)
+        def _():
+            arrived(near_send, chips, ns_sem.at[2 * plane])
+            arrived(part_send, chips, ns_sem.at[2 * plane + 1])
 
 
 def solution(mesh):
@@ -490,8 +504,8 @@
                 pltpu.VMEM((n_chip, CORES, 3, HEAD_SIZE), jnp.float32),
                 pltpu.VMEM((n_req, CORES, 3, HEAD_SIZE), jnp.float32),
                 pltpu.VMEM((n_chip, CORES, 3, HEAD_SIZE), jnp.float32),
-                pltpu.VMEM((n_req, HQ, HEAD_SIZE), jnp.int16),
-                pltpu.VMEM((n_req, 3, HEAD_SIZE), jnp.float32),
+                pltpu.VMEM((2 * n_req, HQ, HEAD_SIZE), jnp.int16),
+                pltpu.VMEM((2 * n_req, 3, HEAD_SIZE), jnp.float32),
                 pltpu.VMEM((CORES * n_kv,) + blob, jnp.float32),
                 pltpu.VMEM((n_kv,) + blob, jnp.float32),
                 pltpu.SemaphoreType.REGULAR,
@@ -503,7 +517,7 @@
                 dma((1,)), dma((n_chip,)),
                 dma((1,)), dma((1,)),
                 dma((1,)), dma((1,)),
-                dma((2,)), dma((2,)),
+                dma((4,)), dma((4,)),
                 dma((1,)), dma((1,)),
             ],
             compiler_params=pltpu.CompilerParams(collective_id=0, has_side_effects=True),

time: 18.2 us -> 17.5 us (0.962)
  Pallas kernels: 17.4 us -> 16.7 us
    pallas_call x1, Pallas kernels: 17.4 us -> 16.7 us  [on_device(): pl.pallas_call(functools.partial(kernel, n_req, n_kv, group), out_shape=p...]
where the time goes in v4:
time: 17.5 us; the launch traced here: 17.3 us
  Pallas kernels  16.7 us (95%)
  local copies, waits for them, and re-layouts  0.62 us (4%)
    pallas_call x1, Pallas kernels, on_device(): pl.pallas_call(functools.partial(kernel, n_req, n_kv, group), out_shape=p...  16.7 us
    unnamed x1, local copies, waits for them, and re-layouts  0.62 us

profile of v4, /device:TPU:0, one launch (start us, length us, event | category | flops | bytes accessed | tf_op | source)
XLA Modules:
  0.0 17.3 jit_solution(4714113404856974863)
XLA Ops:
  0.0 16.7 %shard_map.64 = bf16[32,128]{1,0:T(8,128)(2,1)S(1)} custom-call(s32[6]{0:T(128)} %owner_hbm.1, s32[6]{0:T(128)} %number_hbm.1, s32[32]{0:T(128)} %length_hbm.1, bf16[1,4096]{1,0:T(2,128)(2,1)} %q_hbm.1, bf16[6,128,1024]{2,1,0:T(8,128)(2,1)} %key_hbm.1, bf16[6,128,1024]{2,1,0:T(8,128)(2,1)} %value_hbm.1), custom_call_target="tpu_custom_call" | custom-call | tf_op jit(solution)/shard_map/pallas_call | solution.py:483
  16.7 0.6 %copy.9 = bf16[1,1,32,128]{3,1,2,0:T(2,128)(2,1)} copy(bf16[1,1,32,128]{3,2,1,0:T(8,128)(2,1)S(1)} %bitcast.5) | data formatting | bytes 16384

commit v5 on v4

--- a/solution.py
+++ b/solution.py
@@ -15,7 +15,7 @@
 PAIR = 2 * QUERY_PER_KV
 
 lowest = -1e30
-finest = 1e-30
+finest = 2.0 ** -126
 STEPS = 32767.0
 MESH = pl.DeviceIdType.MESH
 
@@ -131,13 +131,14 @@
     def leaf_column(early):
         pl.semaphore_wait(barrier, n_kv - 1 if early else n_kv)
         pl.semaphore_signal(met_sem, inc=1, device_id=(hub_of[0], my_kv), device_id_type=MESH)
+
+        @pl.when(is_relay)
+        def _():
+            for z in range(n_kv - 2):
+                pl.semaphore_signal(far_sem, inc=1, device_id=(hub_of[0], z), device_id_type=MESH)
+
         remote(q_own, q_col.at[mine], qs_sem.at[0], qr_sem.at[1], (hub_of[0], my_kv)).start()
         send_query(n_kv - 2 if early else n_kv - 1)
-
-        @pl.when(is_relay)
-        def _():
-            for z in range(n_kv - 2):
-                pl.semaphore_signal(far_sem, inc=1, device_id=(hub_of[0], z), device_id_type=MESH)
 
     def leaf_plane():
         pl.semaphore_wait(met_sem, 1)
@@ -286,7 +287,7 @@
             largest[d, b] = jnp.maximum(jnp.max(jnp.abs(blocks), axis=1, keepdims=True), finest)
             summed[d, b] = blocks
         for d, b in batch:
-            coded = jnp.round(summed[d, b] * (STEPS / largest[d, b]))
+            coded = jnp.round(summed[d, b] * (1.0 / largest[d, b]) * STEPS)
             part_send[d, b] = coded.astype(jnp.int32).astype(jnp.int16)
             lanes = [diagonal_to_lanes(column[d, b], on_diagonal) for column in (tops, totals, largest)]
             stat_send[d, b] = jnp.concatenate(lanes, axis=0)
@@ -339,7 +340,7 @@
             stats = [stat_in.at[e, b] for e in range(n_req)]
             tops = [stat[0:1, :] for stat in stats]
             totals = [stat[1:2, :] for stat in stats]
-            steps = [stat[2:3, :] * (1.0 / STEPS) for stat in stats]
+            scales = [stat[2:3, :] for stat in stats]
             picks = [held[b, e] for e in range(n_req)]
             member = [[picks[e] == float(c) for e in range(n_req)] for c in range(group)]
             merged_top, merged_total = [], []
@@ -361,8 +362,8 @@
                 merged_total.append(amount)
             sums = [jnp.zeros((HQ, HEAD_SIZE), jnp.float32) for _ in range(group)]
             for e in range(n_req):
-                coded = sources[e][...].astype(jnp.int32).astype(jnp.float32)
-                scaled = lanes_to_column(factors[e] * steps[e], on_diagonal) * coded
+                coded = sources[e][...].astype(jnp.int32).astype(jnp.float32) * (1.0 / STEPS)
+                scaled = lanes_to_column(factors[e] * scales[e], on_diagonal) * coded
                 pick = jnp.broadcast_to(picks[e], (HQ, HEAD_SIZE))
                 for c in range(group):
                     sums[c] = sums[c] + jnp.where(pick == float(c), scaled, 0.0)
@@ -402,8 +403,8 @@
         arrived(near_in, n_req, nr_sem.at[2 * plane + 1])
         total = jnp.zeros((HQ, HEAD_SIZE), jnp.float32)
         for e in some:
-            step = factors[e] * (near_stat[e, 2:3, :] * (1.0 / STEPS))
-            total = total + lanes_to_column(step, on_diagonal) * near_in[e].astype(jnp.int32).astype(jnp.float32)
+            coded = near_in[e].astype(jnp.int32).astype(jnp.float32) * (1.0 / STEPS)
+            total = total + lanes_to_column(factors[e] * near_stat[e, 2:3, :], on_diagonal) * coded
         merged_in[n_kv - 1 - plane, 0:HQ, :] = total
         merged_in[n_kv - 1 - plane, HQ : HQ + 2, :] = jnp.concatenate([best, amount], axis=0)
 

time: 17.5 us -> 17.5 us (level)
  no operation moved by 1% of the time
where the time goes in v5:
time: 17.5 us; the launch traced here: 17.3 us
  Pallas kernels  16.7 us (95%)
  local copies, waits for them, and re-layouts  0.62 us (4%)
    pallas_call x1, Pallas kernels, on_device(): pl.pallas_call(functools.partial(kernel, n_req, n_kv, group), out_shape=p...  16.7 us
    unnamed x1, local copies, waits for them, and re-layouts  0.62 us

profile of v5, /device:TPU:0, one launch (start us, length us, event | category | flops | bytes accessed | tf_op | source)
XLA Modules:
  0.0 17.3 jit_solution(7668122491594657890)
XLA Ops:
  0.0 16.7 %shard_map.64 = bf16[32,128]{1,0:T(8,128)(2,1)S(1)} custom-call(s32[6]{0:T(128)} %owner_hbm.1, s32[6]{0:T(128)} %number_hbm.1, s32[32]{0:T(128)} %length_hbm.1, bf16[1,4096]{1,0:T(2,128)(2,1)} %q_hbm.1, bf16[6,128,1024]{2,1,0:T(8,128)(2,1)} %key_hbm.1, bf16[6,128,1024]{2,1,0:T(8,128)(2,1)} %value_hbm.1), custom_call_target="tpu_custom_call" | custom-call | tf_op jit(solution)/shard_map/pallas_call | solution.py:484
  16.7 0.6 %copy.9 = bf16[1,1,32,128]{3,1,2,0:T(2,128)(2,1)} copy(bf16[1,1,32,128]{3,2,1,0:T(8,128)(2,1)S(1)} %bitcast.5) | data formatting | bytes 16384

commit v6 on v5

--- a/solution.py
+++ b/solution.py
@@ -194,7 +194,7 @@
             pair.append((index, limit * present, place))
         homes.append(pair)
 
-    edges = [0, max(n_chip // 4, 1), max(3 * n_chip // 4, 1), n_chip]
+    edges = sorted({n_chip * k // 4 for k in range(5)})
     alone = [jnp.logical_and(is_hub, my_chip == c) for c in range(n_chip)]
     met = [jnp.logical_not(own) for own in alone]
 

time: 17.5 us -> 17.5 us (level)
  no operation moved by 1% of the time
where the time goes in v6:
time: 17.5 us; the launch traced here: 17.3 us
  Pallas kernels  16.6 us (95%)
  local copies, waits for them, and re-layouts  0.62 us (4%)
    pallas_call x1, Pallas kernels, on_device(): pl.pallas_call(functools.partial(kernel, n_req, n_kv, group), out_shape=p...  16.6 us
    unnamed x1, local copies, waits for them, and re-layouts  0.62 us

profile of v6, /device:TPU:0, one launch (start us, length us, event | category | flops | bytes accessed | tf_op | source)
XLA Modules:
  0.0 17.3 jit_solution(17566928869956417322)
XLA Ops:
  0.0 16.6 %shard_map.64 = bf16[32,128]{1,0:T(8,128)(2,1)S(1)} custom-call(s32[6]{0:T(128)} %owner_hbm.1, s32[6]{0:T(128)} %number_hbm.1, s32[32]{0:T(128)} %length_hbm.1, bf16[1,4096]{1,0:T(2,128)(2,1)} %q_hbm.1, bf16[6,128,1024]{2,1,0:T(8,128)(2,1)} %key_hbm.1, bf16[6,128,1024]{2,1,0:T(8,128)(2,1)} %value_hbm.1), custom_call_target="tpu_custom_call" | custom-call | tf_op jit(solution)/shard_map/pallas_call | solution.py:484
  16.7 0.6 %copy.9 = bf16[1,1,32,128]{3,1,2,0:T(2,128)(2,1)} copy(bf16[1,1,32,128]{3,2,1,0:T(8,128)(2,1)S(1)} %bitcast.5) | data formatting | bytes 16384
